TPU v7x, 32 devices: a whole 2x2x4 slice. The times are simulated.
32 devices in a mesh: row: 4 (over z), col: 8 (over y, x, core).
Axes of the slice: x: 2, y: 2, z: 4, core: 2. Of those that a mesh axis runs over, the one named last changes fastest.
Arguments:
- a_matrix: float32 [8192, 8192], P('row', 'col'), may hold values from -14 to 30, as said below
- b_matrix: float32 [4096, 4096], P('row', 'col'), may hold values from -14 to 30, as said below
- c_matrix: float32 [8192, 4096], P('row', 'col'), may hold values from -6 to 6
Outputs:
- a_swept: float32 [8192, 8192], P('row', 'col')
- c_swept: float32 [8192, 4096], P('row', 'col')
- b_next: float32 [4096, 4096], P('row', 'col')
Inputs may be any that keep to these rules, and one draw needn't show every extreme that they name: `a_matrix`: symmetric positive definite; its smallest eigenvalue is at least 1. `b_matrix`: symmetric positive definite; its smallest eigenvalue is at least 1.
All inputs are finite; a program needn't handle non-finite values. Where the computation divides by a largest or mean magnitude, that divisor is 1e-20 or more.
Results may differ from a plain program's by a relative error of at most 0.00012.
Values sent between devices are 32-bit elements; how exact they have to be, the bound alone decides.
No kernel may reach another device: no remote copies, remote signals or barrier semaphores. Data moves between devices by JAX's collectives and lax.ppermute only.
A program may use at most 128 MiB of HBM per device.

v0:
```python
import jax
import jax.numpy as jnp
from jax import lax
from jax.sharding import PartitionSpec as P

PANEL = 256
PIVOT_ITERS = 6
STEPS_A = 2
STEPS_B = 16


EXACT = lax.Precision.HIGHEST


def spread(value, axis, source):
    kept = jnp.where(lax.axis_index(axis) == source, value, 0).astype(value.dtype)
    return lax.psum(kept, axis)


def pivot_inverse(pivot):
    order = pivot.shape[0]
    scaling = 1.0 / jnp.sqrt(jnp.diagonal(pivot))
    unit = pivot * scaling[:, None] * scaling[None, :]
    ceiling = jnp.max(jnp.sum(jnp.abs(unit), axis=1))
    approx = jnp.eye(order, dtype=jnp.float32) / ceiling
    for turn in range(PIVOT_ITERS):
        product = jnp.dot(unit, approx, precision=EXACT, preferred_element_type=jnp.float32)
        approx = 2.0 * approx - jnp.dot(
            approx, product, precision=EXACT, preferred_element_type=jnp.float32
        )
    return approx * scaling[:, None] * scaling[None, :]


def frame(matrix, first):
    local_rows = matrix.shape[0]
    row_place = lax.axis_index("row")
    col_place = lax.axis_index("col")
    global_rows = row_place * local_rows + jnp.arange(local_rows, dtype=jnp.int32)
    eye_rows = (global_rows[:, None] == first + jnp.arange(PANEL, dtype=jnp.int32)[None, :]).astype(
        jnp.float32
    )
    return (eye_rows, col_place)


def finish(matrix, solved, rows, first, eye_rows, col_place):
    local_cols = matrix.shape[1]
    offset = first % local_cols
    root_col = first // local_cols
    updated = matrix - jnp.dot(solved, rows, precision=EXACT, preferred_element_type=jnp.float32)
    current = updated[:, offset : offset + PANEL]
    placed = jnp.where(col_place == root_col, eye_rows - solved, current)
    return updated.at[:, offset : offset + PANEL].set(placed)


def a_step(matrix, other, step):
    local_rows, local_cols = matrix.shape
    other_cols = other.shape[1]
    first = step * PANEL
    root_row = first // local_rows
    row_offset = first % local_rows
    root_col = first // local_cols
    col_offset = first % local_cols
    eye_rows, col_place = frame(matrix, first)
    rows = matrix[row_offset : row_offset + PANEL, :]
    other_rows = other[row_offset : row_offset + PANEL, :]
    column = spread(matrix[:, col_offset : col_offset + PANEL], "col", root_col)
    pivot = column[row_offset : row_offset + PANEL, :]
    joined = spread(jnp.concatenate([rows, other_rows, pivot], 1), "row", root_row)
    rows = joined[:, :local_cols]
    other_rows = joined[:, local_cols : local_cols + other_cols]
    pivot = joined[:, local_cols + other_cols :]
    solved = jnp.dot(
        column - eye_rows, pivot_inverse(pivot), precision=EXACT, preferred_element_type=jnp.float32
    )
    new_matrix = finish(matrix, solved, rows, first, eye_rows, col_place)
    new_other = other - jnp.dot(
        solved, other_rows, precision=EXACT, preferred_element_type=jnp.float32
    )
    return (new_matrix, new_other)


def b_step(matrix, step):
    local_rows, local_cols = matrix.shape
    first = step * PANEL
    root_row = first // local_rows
    row_offset = first % local_rows
    root_col = first // local_cols
    col_offset = first % local_cols
    eye_rows, col_place = frame(matrix, first)
    rows = spread(matrix[row_offset : row_offset + PANEL, :], "row", root_row)
    pivot = rows[:, col_offset : col_offset + PANEL]
    column = matrix[:, col_offset : col_offset + PANEL] - eye_rows
    here = jnp.dot(
        column, pivot_inverse(pivot), precision=EXACT, preferred_element_type=jnp.float32
    )
    solved = spread(here, "col", root_col)
    return finish(matrix, solved, rows, first, eye_rows, col_place)


def body(a_matrix, b_matrix, c_matrix):
    b_local = jnp.sum(b_matrix * b_matrix)
    b_squares = lax.psum(b_local, ("row", "col"))
    a_swept, c_swept = (a_matrix, c_matrix)
    for step in range(STEPS_A):
        a_swept, c_swept = a_step(a_swept, c_swept, step)
    b_inverse = b_matrix
    for step in range(STEPS_B):
        b_inverse = b_step(b_inverse, step)
    inv_local = jnp.sum(b_inverse * b_inverse)
    inv_squares = lax.psum(inv_local, ("row", "col"))
    scale = jnp.sqrt(jnp.sqrt(inv_squares / b_squares))
    b_next = 0.5 * (scale * b_matrix + b_inverse / scale)
    return (a_swept, c_swept, b_next)


def solution(mesh):
    return jax.shard_map(
        body,
        mesh=mesh,
        in_specs=(P("row", "col"), P("row", "col"), P("row", "col")),
        out_specs=(P("row", "col"), P("row", "col"), P("row", "col")),
        check_vma=False,
    )
```

profile of v0, /device:TPU:0, one launch (start us, length us, event | category | flops | bytes accessed | tf_op | source)
XLA Modules:
  0.0 2072.1 jit_solution(14993529782840503613)
XLA Ops:
  9.2 43.0 %all-reduce.40.cloned.1.call-done = f32[256,512]{1,0:T(8,128)} async-done(((f32[256,512]{1,0:T(8,128)}), f32[256,512]{1,0:T(8,128)}) %all-reduce.40.cloned.1.call-update) | async-done | bytes 524304 | tf_op jit(solution)/shard_map/psum | solution.py:17
  66.6 56.0 %all-reduce.42.cloned.1.call-done = f32[1024,256]{1,0:T(8,128)} async-done(((f32[1024,256]{1,0:T(8,128)}), f32[1024,256]{1,0:T(8,128)}) %all-reduce.42.cloned.1.call-update) | async-done | bytes 1048592 | tf_op jit(solution)/shard_map/psum | solution.py:17
  129.3 37.8 %all-reduce.44.cloned.1.call-done = f32[256,512]{1,0:T(8,128)} async-done(((f32[256,512]{1,0:T(8,128)}), f32[256,512]{1,0:T(8,128)}) %all-reduce.44.cloned.1.call-update) | async-done | bytes 524304 | tf_op jit(solution)/shard_map/psum | solution.py:17
  180.8 56.6 %all-reduce.46.cloned.1.call-done = f32[1024,256]{1,0:T(8,128)} async-done(((f32[1024,256]{1,0:T(8,128)}), f32[1024,256]{1,0:T(8,128)}) %all-reduce.46.cloned.1.call-update) | async-done | bytes 1048592 | tf_op jit(solution)/shard_map/psum | solution.py:17
  242.9 37.7 %all-reduce.48.cloned.1.call-done = f32[256,512]{1,0:T(8,128)} async-done(((f32[256,512]{1,0:T(8,128)}), f32[256,512]{1,0:T(8,128)}) %all-reduce.48.cloned.1.call-update) | async-done | bytes 524304 | tf_op jit(solution)/shard_map/psum | solution.py:17
  294.4 56.6 %all-reduce.50.cloned.1.call-done = f32[1024,256]{1,0:T(8,128)} async-done(((f32[1024,256]{1,0:T(8,128)}), f32[1024,256]{1,0:T(8,128)}) %all-reduce.50.cloned.1.call-update) | async-done | bytes 1048592 | tf_op jit(solution)/shard_map/psum | solution.py:17
  409.3 56.6 %all-reduce.54.cloned.1.call-done = f32[1024,256]{1,0:T(8,128)} async-done(((f32[1024,256]{1,0:T(8,128)}), f32[1024,256]{1,0:T(8,128)}) %all-reduce.54.cloned.1.call-update) | async-done | bytes 1048592 | tf_op jit(solution)/shard_map/psum | solution.py:17
  522.8 56.6 %all-reduce.58.cloned.1.call-done = f32[1024,256]{1,0:T(8,128)} async-done(((f32[1024,256]{1,0:T(8,128)}), f32[1024,256]{1,0:T(8,128)}) %all-reduce.58.cloned.1.call-update) | async-done | bytes 1048592 | tf_op jit(solution)/shard_map/psum | solution.py:17
  637.5 56.6 %all-reduce.62.cloned.1.call-done = f32[1024,256]{1,0:T(8,128)} async-done(((f32[1024,256]{1,0:T(8,128)}), f32[1024,256]{1,0:T(8,128)}) %all-reduce.62.cloned.1.call-update) | async-done | bytes 1048592 | tf_op jit(solution)/shard_map/psum | solution.py:17
  699.6 37.7 %all-reduce.64.cloned.1.call-done = f32[256,512]{1,0:T(8,128)} async-done(((f32[256,512]{1,0:T(8,128)}), f32[256,512]{1,0:T(8,128)}) %all-reduce.64.cloned.1.call-update) | async-done | bytes 524304 | tf_op jit(solution)/shard_map/psum | solution.py:17
  751.1 56.6 %all-reduce.66.cloned.1.call-done = f32[1024,256]{1,0:T(8,128)} async-done(((f32[1024,256]{1,0:T(8,128)}), f32[1024,256]{1,0:T(8,128)}) %all-reduce.66.cloned.1.call-update) | async-done | bytes 1048592 | tf_op jit(solution)/shard_map/psum | solution.py:17
  866.0 56.6 %all-reduce.70.cloned.1.call-done = f32[1024,256]{1,0:T(8,128)} async-done(((f32[1024,256]{1,0:T(8,128)}), f32[1024,256]{1,0:T(8,128)}) %all-reduce.70.cloned.1.call-update) | async-done | bytes 1048592 | tf_op jit(solution)/shard_map/psum | solution.py:17
  927.9 37.8 %all-reduce.72.cloned.1.call-done = f32[256,512]{1,0:T(8,128)} async-done(((f32[256,512]{1,0:T(8,128)}), f32[256,512]{1,0:T(8,128)}) %all-reduce.72.cloned.1.call-update) | async-done | bytes 524304 | tf_op jit(solution)/shard_map/psum | solution.py:17
  979.5 56.6 %all-reduce.74.cloned.1.call-done = f32[1024,256]{1,0:T(8,128)} async-done(((f32[1024,256]{1,0:T(8,128)}), f32[1024,256]{1,0:T(8,128)}) %all-reduce.74.cloned.1.call-update) | async-done | bytes 1048592 | tf_op jit(solution)/shard_map/psum | solution.py:17
  1094.3 56.6 %all-reduce.78.cloned.1.call-done = f32[1024,256]{1,0:T(8,128)} async-done(((f32[1024,256]{1,0:T(8,128)}), f32[1024,256]{1,0:T(8,128)}) %all-reduce.78.cloned.1.call-update) | async-done | bytes 1048592 | tf_op jit(solution)/shard_map/psum | solution.py:17
  1207.7 56.6 %all-reduce.82.cloned.1.call-done = f32[1024,256]{1,0:T(8,128)} async-done(((f32[1024,256]{1,0:T(8,128)}), f32[1024,256]{1,0:T(8,128)}) %all-reduce.82.cloned.1.call-update) | async-done | bytes 1048592 | tf_op jit(solution)/shard_map/psum | solution.py:17
  1322.5 56.6 %all-reduce.86.cloned.1.call-done = f32[1024,256]{1,0:T(8,128)} async-done(((f32[1024,256]{1,0:T(8,128)}), f32[1024,256]{1,0:T(8,128)}) %all-reduce.86.cloned.1.call-update) | async-done | bytes 1048592 | tf_op jit(solution)/shard_map/psum | solution.py:17
  1384.4 37.8 %all-reduce.88.cloned.1.call-done = f32[256,512]{1,0:T(8,128)} async-done(((f32[256,512]{1,0:T(8,128)}), f32[256,512]{1,0:T(8,128)}) %all-reduce.88.cloned.1.call-update) | async-done | bytes 524304 | tf_op jit(solution)/shard_map/psum | solution.py:17
  1436.0 56.6 %all-reduce.90.cloned.1.call-done = f32[1024,256]{1,0:T(8,128)} async-done(((f32[1024,256]{1,0:T(8,128)}), f32[1024,256]{1,0:T(8,128)}) %all-reduce.90.cloned.1.call-update) | async-done | bytes 1048592 | tf_op jit(solution)/shard_map/psum | solution.py:17
  1550.8 56.6 %all-reduce.94.cloned.1.call-done = f32[1024,256]{1,0:T(8,128)} async-done(((f32[1024,256]{1,0:T(8,128)}), f32[1024,256]{1,0:T(8,128)}) %all-reduce.94.cloned.1.call-update) | async-done | bytes 1048592 | tf_op jit(solution)/shard_map/psum | solution.py:17
  1664.3 69.3 %all-reduce.100.cloned.1.call-done = (f32[2048,256]{1,0:T(8,128)}, f32[1024,256]{1,0:T(8,128)}) async-done(((f32[2048,256]{1,0:T(8,128)}, f32[1024,256]{1,0:T(8,128)}), (f32[2048,256]{1,0:T(8,128)}, f32[1024,256]{1,0:T(8,128)})) %all-reduce.100.cloned.1.call-update) | async-done | bytes 3145744 | tf_op jit(solution)/shard_map/psum | solution.py:17
  1743.4 93.9 %all-reduce.102.cloned.1.call-done = (f32[256,1792]{1,0:T(8,128)}, f32[256,512]{1,0:T(8,128)}) async-done(((f32[256,1792]{1,0:T(8,128)}, f32[256,512]{1,0:T(8,128)}), (f32[256,1792]{1,0:T(8,128)}, f32[256,512]{1,0:T(8,128)})) %all-reduce.102.cloned.1.call-update) | async-done | bytes 2359312 | tf_op jit(solution)/shard_map/psum | solution.py:17
  1893.6 58.5 %all-reduce.98.cloned.1.call-done = (f32[2048,256]{1,0:T(8,128)}, f32[1024,256]{1,0:T(8,128)}) async-done(((f32[2048,256]{1,0:T(8,128)}, f32[1024,256]{1,0:T(8,128)}), (f32[2048,256]{1,0:T(8,128)}, f32[1024,256]{1,0:T(8,128)})) %all-reduce.98.cloned.1.call-update) | async-done | bytes 3145744 | tf_op jit(solution)/shard_map/psum | solution.py:17
  1964.2 41.7 %all-reduce = (f32[]{:T(128)}, f32[]{:T(128)}) all-reduce(f32[]{:T(128)} %multiply_reduce_fusion.1, f32[]{:T(128)} %multiply_reduce_fusion), channel_id=1, replica_groups=mesh['row'=4,'col'=8] {'row','col'}, use_global_device_ids=true, to_apply=%region_76.77 | all-reduce | flops 2 | bytes 16 | tf_op jit(solution)/shard_map/psum | solution.py:110
  (614 shorter events, 752.8 us)
Async XLA Ops:
  9.1 113.5 %all-reduce.42.cloned.1.call-start = ((), (), s32[]{:S(2)}) async-start(), calls=%async_computation.2 | async-start | bytes 2097152 | tf_op jit(solution)/shard_map/psum | solution.py:17
  65.9 101.1 %all-reduce.44.cloned.1.call-start = ((), (), s32[]{:S(2)}) async-start(), calls=%async_computation.3 | async-start | bytes 1048576 | tf_op jit(solution)/shard_map/psum | solution.py:17
  129.0 108.5 %all-reduce.46.cloned.1.call-start = ((), (), s32[]{:S(2)}) async-start(), calls=%async_computation.4 | async-start | bytes 2097152 | tf_op jit(solution)/shard_map/psum | solution.py:17
  242.6 108.5 %all-reduce.50.cloned.1.call-start = ((), (), s32[]{:S(2)}) async-start(), calls=%async_computation.6 | async-start | bytes 2097152 | tf_op jit(solution)/shard_map/psum | solution.py:17
  294.4 101.1 %all-reduce.52.cloned.1.call-start = ((), (), s32[]{:S(2)}) async-start(), calls=%async_computation.7 | async-start | bytes 1048576 | tf_op jit(solution)/shard_map/psum | solution.py:17
  357.5 108.5 %all-reduce.54.cloned.1.call-start = ((), (), s32[]{:S(2)}) async-start(), calls=%async_computation.8 | async-start | bytes 2097152 | tf_op jit(solution)/shard_map/psum | solution.py:17
  471.1 108.3 %all-reduce.58.cloned.1.call-start = ((), (), s32[]{:S(2)}) async-start(), calls=%async_computation.10 | async-start | bytes 2097152 | tf_op jit(solution)/shard_map/psum | solution.py:17
  585.8 108.3 %all-reduce.62.cloned.1.call-start = ((), (), s32[]{:S(2)}) async-start(), calls=%async_computation.12 | async-start | bytes 2097152 | tf_op jit(solution)/shard_map/psum | solution.py:17
  699.2 108.5 %all-reduce.66.cloned.1.call-start = ((), (), s32[]{:S(2)}) async-start(), calls=%async_computation.14 | async-start | bytes 2097152 | tf_op jit(solution)/shard_map/psum | solution.py:17
  751.0 101.2 %all-reduce.68.cloned.1.call-start = ((), (), s32[]{:S(2)}) async-start(), calls=%async_computation.15 | async-start | bytes 1048576 | tf_op jit(solution)/shard_map/psum | solution.py:17
  814.1 108.5 %all-reduce.70.cloned.1.call-start = ((), (), s32[]{:S(2)}) async-start(), calls=%async_computation.16 | async-start | bytes 2097152 | tf_op jit(solution)/shard_map/psum | solution.py:17
  927.7 108.5 %all-reduce.74.cloned.1.call-start = ((), (), s32[]{:S(2)}) async-start(), calls=%async_computation.18 | async-start | bytes 2097152 | tf_op jit(solution)/shard_map/psum | solution.py:17
  979.5 101.0 %all-reduce.76.cloned.1.call-start = ((), (), s32[]{:S(2)}) async-start(), calls=%async_computation.19 | async-start | bytes 1048576 | tf_op jit(solution)/shard_map/psum | solution.py:17
  1042.6 108.3 %all-reduce.78.cloned.1.call-start = ((), (), s32[]{:S(2)}) async-start(), calls=%async_computation.20 | async-start | bytes 2097152 | tf_op jit(solution)/shard_map/psum | solution.py:17
  1156.0 108.3 %all-reduce.82.cloned.1.call-start = ((), (), s32[]{:S(2)}) async-start(), calls=%async_computation.22 | async-start | bytes 2097152 | tf_op jit(solution)/shard_map/psum | solution.py:17
  1207.7 101.0 %all-reduce.84.cloned.1.call-start = ((), (), s32[]{:S(2)}) async-start(), calls=%async_computation.23 | async-start | bytes 1048576 | tf_op jit(solution)/shard_map/psum | solution.py:17
  1270.8 108.3 %all-reduce.86.cloned.1.call-start = ((), (), s32[]{:S(2)}) async-start(), calls=%async_computation.24 | async-start | bytes 2097152 | tf_op jit(solution)/shard_map/psum | solution.py:17
  1384.2 108.5 %all-reduce.90.cloned.1.call-start = ((), (), s32[]{:S(2)}) async-start(), calls=%async_computation.26 | async-start | bytes 2097152 | tf_op jit(solution)/shard_map/psum | solution.py:17
  1436.0 101.0 %all-reduce.92.cloned.1.call-start = ((), (), s32[]{:S(2)}) async-start(), calls=%async_computation.27 | async-start | bytes 1048576 | tf_op jit(solution)/shard_map/psum | solution.py:17
  1499.1 108.3 %all-reduce.94.cloned.1.call-start = ((), (), s32[]{:S(2)}) async-start(), calls=%async_computation.28 | async-start | bytes 2097152 | tf_op jit(solution)/shard_map/psum | solution.py:17
  1612.5 121.1 %all-reduce.100.cloned.1.call-start = ((), (), s32[]{:S(2)}) async-start(), calls=%async_computation.31 | async-start | bytes 6291456 | tf_op jit(solution)/shard_map/psum | solution.py:17
  1664.3 173.0 %all-reduce.102.cloned.1.call-start = ((), (), s32[]{:S(2)}) async-start(), calls=%async_computation.32 | async-start | bytes 4718592 | tf_op jit(solution)/shard_map/psum | solution.py:17
  1742.5 209.7 %all-reduce.98.cloned.1.call-start = ((), (), s32[]{:S(2)}) async-start(), calls=%async_computation.30 | async-start | bytes 6291456 | tf_op jit(solution)/shard_map/psum | solution.py:17
  1883.6 151.1 %all-reduce.38.cloned.1.call-start = ((), (), s32[]{:S(2)}) async-start(), calls=%async_computation | async-start | bytes 3670016 | tf_op jit(solution)/shard_map/psum | solution.py:17
  (73 other events, 1103.8 us)
Sparse Core Ops, SparseCore 0:
  10.9 41.2 all-reduce.39
  66.0 56.5 all-reduce.41
  180.9 56.5 all-reduce.45
  242.7 37.8 all-reduce.47
  294.5 56.5 all-reduce.49
  409.4 56.5 all-reduce.53
  522.8 56.5 all-reduce.57
  637.6 56.5 all-reduce.61
  699.4 37.8 all-reduce.63
  751.1 56.5 all-reduce.65
  814.2 37.8 all-reduce.67
  866.0 56.5 all-reduce.69
  927.8 37.8 all-reduce.71
  979.6 56.5 all-reduce.73
  1094.4 56.5 all-reduce.77
  1207.8 56.5 all-reduce.81
  1322.5 56.5 all-reduce.85
  1436.1 56.5 all-reduce.89
  1550.8 56.4 all-reduce.93
  1612.6 37.8 all-reduce.95
  1664.4 69.1 all-reduce.99
  1742.6 94.6 all-reduce.101
  1883.7 68.3 all-reduce.97
  1956.0 78.6 all-reduce.37
  (9 shorter events, 339.7 us)
where the time goes:
time: 2080 us; the launch traced here: 2070 us
  waiting for transfers between devices  1610 us (77%)
  matrix products  226 us (11%)
  local copies, waits for them, and re-layouts  86.6 us (4%)
  other arithmetic  75.1 us (4%)
  blocking collectives  41.7 us (2%)
  between operations  32 us (2%)
    psum x33, waiting for transfers between devices, spread(): return lax.psum(kept, axis)  1600 us
    dot_general x18, matrix products, finish(): jnp.dot(solved, rows, precision=EXACT, preferred_element_type=jnp.float32)  76.9 us
    dot_general x108, matrix products, pivot_inverse(): jnp.dot(unit, approx, precision=EXACT, preferred_element_type=jnp.float32)  60.3 us
    gather x18, local copies, waits for them, and re-layouts, pivot_inverse(): scaling = 1.0 / jnp.sqrt(jnp.diagonal(pivot))  42.2 us
    psum x1, blocking collectives, body(): inv_squares = lax.psum(inv_local, ('row', 'col'))  41.7 us
  transfers between devices with their start and end apart: 33, of which 33 were waited for; matrix products, arithmetic and copies ran while one was open for 1% of the time, Pallas kernels for 0%

commit v1 on v0

v1 whole, which is shorter than its diff:
```python
import jax
import jax.numpy as jnp
from jax import lax
from jax.sharding import PartitionSpec as P

PANEL = 256
PIVOT_ITERS = 6
STEPS_A = 2
STEPS_B = 16


EXACT = lax.Precision.HIGHEST
CLOSE = lax.Precision.HIGH


def spread(value, axis, source):
    kept = jnp.where(lax.axis_index(axis) == source, value, 0).astype(value.dtype)
    return lax.psum(kept, axis)


def pivot_inverse(pivot):
    order = pivot.shape[0]
    unit_square = jnp.eye(order, dtype=jnp.float32)
    scaling = 1.0 / jnp.sqrt(jnp.sum(pivot * unit_square, axis=1))
    unit = pivot * scaling[:, None] * scaling[None, :]
    ceiling = jnp.max(jnp.sum(jnp.abs(unit), axis=1))
    approx = jnp.eye(order, dtype=jnp.float32) / ceiling
    for turn in range(PIVOT_ITERS):
        product = jnp.dot(unit, approx, precision=EXACT, preferred_element_type=jnp.float32)
        approx = 2.0 * approx - jnp.dot(
            approx, product, precision=EXACT, preferred_element_type=jnp.float32
        )
    return approx * scaling[:, None] * scaling[None, :]


def mul(left, right, dims, precision):
    return lax.dot_general(
        left, right, (dims, ((), ())), precision=precision, preferred_element_type=jnp.float32
    )


def sweep_panel(block, panel, places):
    order = block.shape[0]
    index = jnp.arange(order, dtype=jnp.int32)
    eye = (index[:, None] == jnp.concatenate([index, places])[None, :]).astype(jnp.float32)
    both = jnp.concatenate([block, panel], 1)
    for start in range(0, order, PANEL):
        stop = start + PANEL
        inverse = pivot_inverse(both[start:stop, start:stop].T)
        solved = mul(inverse, both[start:stop] - eye[start:stop], ((0,), (0,)), EXACT)
        updated = both - mul(both[:, start:stop], solved, ((1,), (0,)), CLOSE)
        both = jnp.concatenate(
            [updated[:start], eye[start:stop] - solved, updated[stop:]], 0
        )
    return both[:, order:], eye[:, order:]


def a_sweep(matrix, other):
    local_rows, local_cols = matrix.shape
    other_cols = other.shape[1]
    order = STEPS_A * PANEL
    row_place = lax.axis_index("row")
    col_place = lax.axis_index("col")
    panel = spread(matrix[:, :order], "col", 0)
    joined = spread(
        jnp.concatenate([matrix[:order], other[:order], panel[:order]], 1), "row", 0
    )
    rows = joined[:, : local_cols + other_cols]
    block = joined[:, local_cols + other_cols :].T
    places = row_place * local_rows + jnp.arange(local_rows, dtype=jnp.int32)
    swept, eye = sweep_panel(block, panel.T, places)
    solved = eye - swept
    new_matrix = matrix - mul(solved, rows[:, :local_cols], ((0,), (0,)), CLOSE)
    new_other = other - mul(solved, rows[:, local_cols:], ((0,), (0,)), CLOSE)
    front = jnp.where(col_place == 0, swept.T, new_matrix[:, :order])
    return new_matrix.at[:, :order].set(front), new_other


def b_sweep(matrix, row_count, col_count):
    local_rows, local_cols = matrix.shape
    order = min(local_rows, local_cols)
    steps = STEPS_B * PANEL // order
    row_part = order // row_count
    col_part = order // col_count
    row_place = lax.axis_index("row")
    col_place = lax.axis_index("col")
    dealt = matrix.T.reshape(local_cols // order, col_count, col_part, local_rows)
    dealt = lax.all_to_all(dealt, "col", 1, 0, tiled=True).reshape(local_cols, local_rows)
    dealt = dealt.T.reshape(local_rows // order, row_count, row_part, local_cols)
    dealt = lax.all_to_all(dealt, "row", 1, 0, tiled=True).reshape(local_rows, local_cols)
    index = jnp.arange(local_rows, dtype=jnp.int32)
    for step in range(steps):
        top = step * row_part
        left = step * col_part
        panel = lax.all_gather(dealt[:, left : left + col_part].T, "col", axis=0, tiled=True)
        joined = jnp.concatenate(
            [dealt[top : top + row_part], panel[:, top : top + row_part].T], 1
        )
        joined = lax.all_gather(joined, "row", axis=0, tiled=True)
        rows = joined[:, :local_cols]
        block = joined[:, local_cols:].T
        inside = (index >= top) & (index < top + row_part)
        places = jnp.where(inside, index - top + row_place * row_part, -1)
        swept, eye = sweep_panel(block, panel, places)
        updated = dealt + mul(swept - eye, rows, ((0,), (0,)), CLOSE)
        own = lax.dynamic_slice_in_dim(swept, col_place * col_part, col_part, 0).T
        dealt = updated.at[:, left : left + col_part].set(own)
    back = dealt.reshape(steps, 1, row_part, local_cols)
    back = lax.all_to_all(back, "row", 0, 1, tiled=True).reshape(local_rows, local_cols)
    back = back.T.reshape(steps, 1, col_part, local_rows)
    back = lax.all_to_all(back, "col", 0, 1, tiled=True).reshape(local_cols, local_rows)
    return back.T


def solution(mesh):
    row_count = mesh.shape["row"]
    col_count = mesh.shape["col"]

    def body(a_matrix, b_matrix, c_matrix):
        b_local = jnp.sum(b_matrix * b_matrix)
        a_swept, c_swept = a_sweep(a_matrix, c_matrix)
        b_inverse = b_sweep(b_matrix, row_count, col_count)
        inv_local = jnp.sum(b_inverse * b_inverse)
        sums = lax.psum(jnp.stack([b_local, inv_local]), ("row", "col"))
        scale = jnp.sqrt(jnp.sqrt(sums[1] / sums[0]))
        b_next = 0.5 * (scale * b_matrix + b_inverse / scale)
        return (a_swept, c_swept, b_next)

    return jax.shard_map(
        body,
        mesh=mesh,
        in_specs=(P("row", "col"), P("row", "col"), P("row", "col")),
        out_specs=(P("row", "col"), P("row", "col"), P("row", "col")),
        check_vma=False,
    )
```

time: 2080 us -> 1520 us (0.73)
  waiting for transfers between devices: 1610 us -> 706 us
  local copies, waits for them, and re-layouts: 86.6 us -> 229 us
  blocking collectives: 41.7 us -> 121 us
  matrix products: 226 us -> 290 us
  other arithmetic: 75.1 us -> 115 us
    psum x33 -> x2, waiting for transfers between devices: 1600 us -> 165 us  [spread(): return lax.psum(kept, axis)]
    all_gather x0 -> x16, waiting for transfers between devices: none -> 524 us  [the longest x8 332 us: b_sweep(): joined = lax.all_gather(joined, 'row', axis=0, tiled=True)]
    all_to_all x0 -> x2, blocking collectives: none -> 84 us  [the longest x1 52.3 us: b_sweep(): lax.all_to_all(dealt, 'row', 1, 0, tiled=True)]
    dot_general x1 -> x18, local copies, waits for them, and re-layouts: 1.99 us -> 55.2 us  [mul(): lax.dot_general(left, right, (dims, ((), ())), precision=precision, prefe...]
    gather x18 -> x0, local copies, waits for them, and re-layouts: 42.2 us -> none  [pivot_inverse(): scaling = 1.0 / jnp.sqrt(jnp.diagonal(pivot))]
    dot_general x108, matrix products: 60.3 us -> 97.6 us  [pivot_inverse(): jnp.dot(unit, approx, precision=EXACT, preferred_element_type=jnp.float32)]
    unnamed x124 -> x226, local copies, waits for them, and re-layouts: 19.3 us -> 55.1 us
    transpose x0 -> x35, local copies, waits for them, and re-layouts: none -> 33.9 us  [the longest x16 17.4 us: b_sweep(): dealt[:, left:left + col_part]]
  transfers between devices with their start and end apart: 33 -> 20, of which waited for: 33 -> 20; matrix products, arithmetic and copies ran while one was open for 1% -> 12% of each run, Pallas kernels for 0% -> 0%
where the time goes in v1:
time: 1520 us; the launch traced here: 1500 us
  waiting for transfers between devices  706 us (46%)
  matrix products  290 us (19%)
  local copies, waits for them, and re-layouts  229 us (15%)
  blocking collectives  121 us (8%)
  other arithmetic  115 us (8%)
  between operations  31.5 us (2%)
    all_gather x8, waiting for transfers between devices, b_sweep(): joined = lax.all_gather(joined, 'row', axis=0, tiled=True)  332 us
    all_gather x8, waiting for transfers between devices, b_sweep(): lax.all_gather(dealt[:, left:left + col_part].T, 'col', axis=0, tiled=True)  192 us
    psum x2, waiting for transfers between devices, spread(): return lax.psum(kept, axis)  165 us
    dot_general x46, matrix products, mul(): lax.dot_general(left, right, (dims, ((), ())), precision=precision, prefe...  149 us
    dot_general x108, matrix products, pivot_inverse(): jnp.dot(unit, approx, precision=EXACT, preferred_element_type=jnp.float32)  97.6 us
    dot_general x18, local copies, waits for them, and re-layouts, mul(): lax.dot_general(left, right, (dims, ((), ())), precision=precision, prefe...  55.2 us
    unnamed x226, local copies, waits for them, and re-layouts  55.1 us
    all_to_all x1, blocking collectives, b_sweep(): lax.all_to_all(dealt, 'row', 1, 0, tiled=True)  52.3 us
  transfers between devices with their start and end apart: 20, of which 20 were waited for; matrix products, arithmetic and copies ran while one was open for 12% of the time, Pallas kernels for 0%

profile of v1, /device:TPU:0, one launch (start us, length us, event | category | flops | bytes accessed | tf_op | source)
XLA Modules:
  0.0 1503.8 jit_solution(638320156755108339)
XLA Ops:
  9.2 31.7 %all_to_all.48 = f32[1,8,64,1024]{3,2,0,1:T(8,128)} all-to-all(f32[1,8,64,1024]{3,2,0,1:T(8,128)S(1)} %bitcast.702), channel_id=1, replica_groups=mesh['row'=4,'col'=8] {'col'}, dimensions={1} | all-to-all | bytes 4194304 | tf_op jit(solution)/shard_map/all_to_all | solution.py:88
  43.0 52.3 %all_to_all.49 = f32[2,4,128,512]{3,2,0,1:T(8,128)S(1)} all-to-all(f32[2,4,128,512]{3,2,0,1:T(8,128)S(1)} %copy.155), channel_id=1, replica_groups=mesh['row'=4,'col'=8] {'row'}, dimensions={1} | all-to-all | bytes 4194304 | tf_op jit(solution)/shard_map/all_to_all | solution.py:90
  96.7 25.7 %all-gather.17.cloned.1.call-done = f32[512,1024]{1,0:T(8,128)} async-done(((f32[64,1024]{1,0:T(8,128)}), f32[512,1024]{1,0:T(8,128)}) %all-gather.17.cloned.1.call-update) | async-done | bytes 2097168 | tf_op jit(solution)/shard_map/all_gather | solution.py:95
  126.9 44.2 %all-gather.19.cloned.1.call-done = f32[512,1024]{1,0:T(8,128)} async-done(((f32[128,1024]{1,0:T(8,128)}), f32[512,1024]{1,0:T(8,128)}) %all-gather.19.cloned.1.call-update) | async-done | bytes 2097168 | tf_op jit(solution)/shard_map/all_gather | solution.py:99
  230.8 25.7 %all-gather.21.cloned.1.call-done = f32[512,1024]{1,0:T(8,128)} async-done(((f32[64,1024]{1,0:T(8,128)}), f32[512,1024]{1,0:T(8,128)}) %all-gather.21.cloned.1.call-update) | async-done | bytes 2097168 | tf_op jit(solution)/shard_map/all_gather | solution.py:95
  260.5 44.7 %all-gather.23.cloned.1.call-done = f32[512,1024]{1,0:T(8,128)} async-done(((f32[128,1024]{1,0:T(8,128)}), f32[512,1024]{1,0:T(8,128)}) %all-gather.23.cloned.1.call-update) | async-done | bytes 2097168 | tf_op jit(solution)/shard_map/all_gather | solution.py:99
  365.0 25.7 %all-gather.25.cloned.1.call-done = f32[512,1024]{1,0:T(8,128)} async-done(((f32[64,1024]{1,0:T(8,128)}), f32[512,1024]{1,0:T(8,128)}) %all-gather.25.cloned.1.call-update) | async-done | bytes 2097168 | tf_op jit(solution)/shard_map/all_gather | solution.py:95
  395.0 44.5 %all-gather.27.cloned.1.call-done = f32[512,1024]{1,0:T(8,128)} async-done(((f32[128,1024]{1,0:T(8,128)}), f32[512,1024]{1,0:T(8,128)}) %all-gather.27.cloned.1.call-update) | async-done | bytes 2097168 | tf_op jit(solution)/shard_map/all_gather | solution.py:99
  498.8 25.7 %all-gather.29.cloned.1.call-done = f32[512,1024]{1,0:T(8,128)} async-done(((f32[64,1024]{1,0:T(8,128)}), f32[512,1024]{1,0:T(8,128)}) %all-gather.29.cloned.1.call-update) | async-done | bytes 2097168 | tf_op jit(solution)/shard_map/all_gather | solution.py:95
  528.6 44.7 %all-gather.31.cloned.1.call-done = f32[512,1024]{1,0:T(8,128)} async-done(((f32[128,1024]{1,0:T(8,128)}), f32[512,1024]{1,0:T(8,128)}) %all-gather.31.cloned.1.call-update) | async-done | bytes 2097168 | tf_op jit(solution)/shard_map/all_gather | solution.py:99
  633.2 25.7 %all-gather.33.cloned.1.call-done = f32[512,1024]{1,0:T(8,128)} async-done(((f32[64,1024]{1,0:T(8,128)}), f32[512,1024]{1,0:T(8,128)}) %all-gather.33.cloned.1.call-update) | async-done | bytes 2097168 | tf_op jit(solution)/shard_map/all_gather | solution.py:95
  662.9 44.7 %all-gather.35.cloned.1.call-done = f32[512,1024]{1,0:T(8,128)} async-done(((f32[128,1024]{1,0:T(8,128)}), f32[512,1024]{1,0:T(8,128)}) %all-gather.35.cloned.1.call-update) | async-done | bytes 2097168 | tf_op jit(solution)/shard_map/all_gather | solution.py:99
  767.0 25.7 %all-gather.37.cloned.1.call-done = f32[512,1024]{1,0:T(8,128)} async-done(((f32[64,1024]{1,0:T(8,128)}), f32[512,1024]{1,0:T(8,128)}) %all-gather.37.cloned.1.call-update) | async-done | bytes 2097168 | tf_op jit(solution)/shard_map/all_gather | solution.py:95
  796.9 44.5 %all-gather.39.cloned.1.call-done = f32[512,1024]{1,0:T(8,128)} async-done(((f32[128,1024]{1,0:T(8,128)}), f32[512,1024]{1,0:T(8,128)}) %all-gather.39.cloned.1.call-update) | async-done | bytes 2097168 | tf_op jit(solution)/shard_map/all_gather | solution.py:99
  905.9 20.9 %all-gather.41.cloned.1.call-done = f32[512,1024]{1,0:T(8,128)} async-done(((f32[64,1024]{1,0:T(8,128)}), f32[512,1024]{1,0:T(8,128)}) %all-gather.41.cloned.1.call-update) | async-done | bytes 2097168 | tf_op jit(solution)/shard_map/all_gather | solution.py:95
  938.2 73.2 %all-reduce.3.cloned.1.call-done = f32[2048,512]{1,0:T(8,128)} async-done(((f32[2048,512]{1,0:T(8,128)}), f32[2048,512]{1,0:T(8,128)}) %all-reduce.3.cloned.1.call-update) | async-done | bytes 4194320 | tf_op jit(solution)/shard_map/psum | solution.py:18
  1017.4 41.2 %all-gather.43.cloned.1.call-done = f32[512,1024]{1,0:T(8,128)} async-done(((f32[128,1024]{1,0:T(8,128)}), f32[512,1024]{1,0:T(8,128)}) %all-gather.43.cloned.1.call-update) | async-done | bytes 2097168 | tf_op jit(solution)/shard_map/all_gather | solution.py:99
  1123.7 91.5 %all-reduce.5.cloned.1.call-done = f32[512,2048]{1,0:T(8,128)} async-done(((f32[512,2048]{1,0:T(8,128)}), f32[512,2048]{1,0:T(8,128)}) %all-reduce.5.cloned.1.call-update) | async-done | bytes 4194320 | tf_op jit(solution)/shard_map/psum | solution.py:18
  1227.0 16.7 %all-gather.45.cloned.1.call-done = f32[512,1024]{1,0:T(8,128)} async-done(((f32[64,1024]{1,0:T(8,128)}), f32[512,1024]{1,0:T(8,128)}) %all-gather.45.cloned.1.call-update) | async-done | bytes 2097168 | tf_op jit(solution)/shard_map/all_gather | solution.py:95
  1271.6 24.0 %all-gather.47.cloned.1.call-done = f32[512,1024]{1,0:T(8,128)} async-done(((f32[128,1024]{1,0:T(8,128)}), f32[512,1024]{1,0:T(8,128)}) %all-gather.47.cloned.1.call-update) | async-done | bytes 2097168 | tf_op jit(solution)/shard_map/all_gather | solution.py:99
  1391.4 13.3 all-to-all-done.2
  1418.6 11.6 convolution_subtract_fusion
  1443.8 9.8 convolution_subtract_fusion.9
  1453.6 36.8 %psum.23 = f32[2]{0:T(128)S(1)} all-reduce(f32[2]{0:T(128)S(1)} %pad_maximum_fusion.35), channel_id=1, replica_groups=mesh['row'=4,'col'=8] {'row','col'}, use_global_device_ids=true, to_apply=%region_66.67 | all-reduce | flops 2 | bytes 16 | tf_op jit(solution)/shard_map/psum | solution.py:124
  (760 shorter events, 627.9 us)
Async XLA Ops:
  7.2 115.2 %all-gather.17.cloned.1.call-start = ((), (), s32[]{:S(2)}) async-start(), calls=%async_computation.6 | async-start | bytes 2359296 | tf_op jit(solution)/shard_map/all_gather | solution.py:95
  9.1 31.7 %copy-start.55 = (f32[1024,512]{0,1:T(8,128)}, f32[1024,512]{0,1:T(8,128)S(1)}, u32[]{:S(2)}) copy-start(f32[1024,512]{0,1:T(8,128)S(1)} %copy.152) | copy-start | bytes 6291460
  96.5 74.6 %all-gather.19.cloned.1.call-start = ((), (), s32[]{:S(2)}) async-start(), calls=%async_computation.7 | async-start | bytes 2621440 | tf_op jit(solution)/shard_map/all_gather | solution.py:99
  125.3 131.2 %all-gather.21.cloned.1.call-start = ((), (), s32[]{:S(2)}) async-start(), calls=%async_computation.8 | async-start | bytes 2359296 | tf_op jit(solution)/shard_map/all_gather | solution.py:95
  229.8 75.4 %all-gather.23.cloned.1.call-start = ((), (), s32[]{:S(2)}) async-start(), calls=%async_computation.9 | async-start | bytes 2621440 | tf_op jit(solution)/shard_map/all_gather | solution.py:99
  259.4 131.3 %all-gather.25.cloned.1.call-start = ((), (), s32[]{:S(2)}) async-start(), calls=%async_computation.10 | async-start | bytes 2359296 | tf_op jit(solution)/shard_map/all_gather | solution.py:95
  364.0 75.4 %all-gather.27.cloned.1.call-start = ((), (), s32[]{:S(2)}) async-start(), calls=%async_computation.11 | async-start | bytes 2621440 | tf_op jit(solution)/shard_map/all_gather | solution.py:99
  393.6 130.9 %all-gather.29.cloned.1.call-start = ((), (), s32[]{:S(2)}) async-start(), calls=%async_computation.12 | async-start | bytes 2359296 | tf_op jit(solution)/shard_map/all_gather | solution.py:95
  497.8 75.4 %all-gather.31.cloned.1.call-start = ((), (), s32[]{:S(2)}) async-start(), calls=%async_computation.13 | async-start | bytes 2621440 | tf_op jit(solution)/shard_map/all_gather | solution.py:99
  527.4 131.5 %all-gather.33.cloned.1.call-start = ((), (), s32[]{:S(2)}) async-start(), calls=%async_computation.14 | async-start | bytes 2359296 | tf_op jit(solution)/shard_map/all_gather | solution.py:95
  632.1 75.4 %all-gather.35.cloned.1.call-start = ((), (), s32[]{:S(2)}) async-start(), calls=%async_computation.15 | async-start | bytes 2621440 | tf_op jit(solution)/shard_map/all_gather | solution.py:99
  661.8 130.9 %all-gather.37.cloned.1.call-start = ((), (), s32[]{:S(2)}) async-start(), calls=%async_computation.16 | async-start | bytes 2359296 | tf_op jit(solution)/shard_map/all_gather | solution.py:95
  766.0 75.4 %all-gather.39.cloned.1.call-start = ((), (), s32[]{:S(2)}) async-start(), calls=%async_computation.17 | async-start | bytes 2621440 | tf_op jit(solution)/shard_map/all_gather | solution.py:99
  795.6 131.3 %all-gather.41.cloned.1.call-start = ((), (), s32[]{:S(2)}) async-start(), calls=%async_computation.18 | async-start | bytes 2359296 | tf_op jit(solution)/shard_map/all_gather | solution.py:95
  900.1 111.3 %all-reduce.3.cloned.1.call-start = ((), (), s32[]{:S(2)}) async-start(), calls=%async_computation.4 | async-start | bytes 8388608 | tf_op jit(solution)/shard_map/psum | solution.py:18
  904.9 153.7 %all-gather.43.cloned.1.call-start = ((), (), s32[]{:S(2)}) async-start(), calls=%async_computation.19 | async-start | bytes 2621440 | tf_op jit(solution)/shard_map/all_gather | solution.py:99
  929.7 285.5 %all-reduce.5.cloned.1.call-start = ((), (), s32[]{:S(2)}) async-start(), calls=%async_computation.5 | async-start | bytes 8388608 | tf_op jit(solution)/shard_map/psum | solution.py:18
  1016.9 226.8 %all-gather.45.cloned.1.call-start = ((), (), s32[]{:S(2)}) async-start(), calls=%async_computation.20 | async-start | bytes 2359296 | tf_op jit(solution)/shard_map/all_gather | solution.py:95
  1120.1 175.4 %all-gather.47.cloned.1.call-start = ((), (), s32[]{:S(2)}) async-start(), calls=%async_computation.21 | async-start | bytes 2621440 | tf_op jit(solution)/shard_map/all_gather | solution.py:99
  1351.4 53.2 %all-to-all-start.2 = ((f32[8,1,128,512]{3,2,1,0:T(8,128)}), f32[8,1,128,512]{3,2,1,0:T(8,128)}, u32[]{:S(2)}, u32[]{:S(2)}) async-start(f32[8,1,128,512]{3,2,1,0:T(8,128)} %bitcast.706), calls=%async_computation.2 | async-start | bytes 4194304 | tf_op jit(solution)/shard_map/all_to_all | solution.py:109
  1357.7 10.8 slice-start
  1408.4 31.3 %all-to-all-start.3 = ((f32[8,1,64,1024]{3,2,1,0:T(8,128)}), f32[8,1,64,1024]{3,2,1,0:T(8,128)}, u32[]{:S(2)}, u32[]{:S(2)}) async-start(f32[8,1,64,1024]{3,2,1,0:T(8,128)} %bitcast.72), calls=%async_computation.3 | async-start | bytes 4194304 | tf_op jit(solution)/shard_map/all_to_all | solution.py:111
  1416.1 14.1 copy-start.3
  1430.2 13.5 copy-start.5
  (109 other events, 289.6 us)
Sparse Core Ops, SparseCore 0:
  96.6 25.7 all-gather.16
  125.4 45.6 all-gather.18
  229.9 26.5 all-gather.20
  259.5 45.6 all-gather.22
  364.1 26.5 all-gather.24
  393.8 45.6 all-gather.26
  497.9 26.5 all-gather.28
  527.5 45.6 all-gather.30
  632.3 26.5 all-gather.32
  661.9 45.6 all-gather.34
  766.1 26.5 all-gather.36
  795.7 45.6 all-gather.38
  900.2 26.5 all-gather.40
  930.5 80.8 all-reduce.2
  1012.8 45.7 all-gather.42
  1061.4 153.7 all-reduce.4
  1216.9 26.7 all-gather.44
  1249.9 45.6 all-gather.46
